TPU v7x, 32 devices: a whole 2x2x4 slice. The times are simulated.
32 devices in a mesh: slab: 4 (over y, core), wide: 8 (over z, x).
Axes of the slice: x: 2, y: 2, z: 4, core: 2. Of those that a mesh axis runs over, the one named last changes fastest.
Arguments:
- spectrum: float32 [1152, 32, 128], P('wide', 'slab'), may hold values from 0 to 1
- sea_mask: int32 [32, 128], P('slab'), may hold values 0 or 1
- courant: float32 [32], replicated, may hold values from 0.05 to 0.7
- slot_owner: int32 [1152], replicated, may hold values from 0 to 1151, each once
- coupling: bfloat16 [1152, 1152], replicated, may hold values from -0.1875 to 0.1875
Outputs:
- evolved: float32 [1152, 32, 128], P('wide', 'slab')
Inputs may be any that keep to these rules, and one draw needn't show every extreme that they name: `slot_owner`: each component occurs in exactly one slot; component f * 36 + d has direction d and frequency f. `sea_mask`: 1 marks a sea point.
All inputs are finite; a program needn't handle non-finite values. No bound on the sum of `sea_mask` on one device may be relied on, other than what follows from the above.
Results may differ from a plain program's by a relative error of at most 0.0015.
Values sent between devices are 32-bit elements; how exact they have to be, the bound alone decides.
No kernel may reach another device: no remote copies, remote signals or barrier semaphores. Data moves between devices by JAX's collectives and lax.ppermute only.
A program may use at most 64 MiB of HBM per device.

v0:
```python
import math

import jax
import jax.numpy as jnp
from jax import lax
from jax.sharding import PartitionSpec as P

ND = 36
STEPS = 2


time_step = 0.5


def extended(cells, sides, width):
    for axis, dim in sides:
        count = lax.axis_size(axis)
        ends = count - 1
        head = lax.slice_in_dim(cells, 0, width, axis=dim)
        tail = lax.slice_in_dim(cells, cells.shape[dim] - width, cells.shape[dim], axis=dim)
        cells = jnp.concatenate(
            [
                lax.ppermute(tail, axis, [(i, (i + 1) % count) for i in range(ends)]),
                cells,
                lax.ppermute(head, axis, [((i + 1) % count, i) for i in range(ends)]),
            ],
            axis=dim,
        )
    return cells


def velocities(slot_owner, courant):
    band_count = courant.shape[0]
    heading = slot_owner % ND
    freq_band = slot_owner // ND
    picked = freq_band[:, None] == jnp.arange(band_count, dtype=jnp.int32)[None, :]
    wave_speed = jnp.sum(jnp.where(picked, courant[None, :], 0.0), axis=1)
    wave_angle = heading.astype(jnp.float32) * (2.0 * math.pi / ND)
    return (wave_speed * jnp.cos(wave_angle), wave_speed * jnp.sin(wave_angle))


def combine_sides(energy, west_side, east_side, south_side, north_side, east_speed, north_speed):
    east_speed = east_speed[:, None, None]
    north_speed = north_speed[:, None, None]
    remain = 1.0 - jnp.abs(east_speed) - jnp.abs(north_speed)
    result = remain * energy + jnp.maximum(east_speed, 0.0) * west_side
    result = result + jnp.maximum(-east_speed, 0.0) * east_side
    result = result + jnp.maximum(north_speed, 0.0) * south_side
    return result + jnp.maximum(-north_speed, 0.0) * north_side


def advect(energy, padded, east_speed, north_speed):
    west_side = jnp.roll(energy, 1, axis=2)
    east_side = jnp.roll(energy, -1, axis=2)
    return combine_sides(
        energy, west_side, east_side, padded[:, :-2, :], padded[:, 2:, :], east_speed, north_speed
    )


def interact(moved, slot_table):
    slot_count = moved.shape[0]
    flattened = moved.reshape(slot_count, -1)
    rounded = flattened.astype(jnp.bfloat16)
    square = (flattened * flattened).astype(jnp.bfloat16)
    gain_term = flattened * jnp.dot(slot_table, rounded, preferred_element_type=jnp.float32)
    loss_term = lax.dot_general(
        slot_table, square, (((0,), (0,)), ((), ())), preferred_element_type=jnp.float32
    )
    updated = jnp.maximum(flattened + time_step * (gain_term - loss_term), 0.0)
    return updated.reshape(moved.shape)


def body(spectrum, sea_mask, courant, slot_owner, coupling):
    slot_count = spectrum.shape[0]
    wide_index = lax.axis_index("wide")
    sea_float = sea_mask.astype(jnp.float32)
    slot_table = jnp.take(jnp.take(coupling, slot_owner, axis=0), slot_owner, axis=1)
    energy = spectrum * sea_float[None]
    own_slots = lax.dynamic_slice_in_dim(slot_owner, wide_index * slot_count, slot_count, 0)
    east_speed, north_speed = velocities(own_slots, courant)
    for repeat in range(STEPS):
        padded = extended(energy, (("slab", 1),), 1)
        moved = advect(energy, padded, east_speed, north_speed)
        energy = (
            lax.all_to_all(
                interact(
                    lax.all_to_all(moved, "wide", split_axis=1, concat_axis=0, tiled=True),
                    slot_table,
                ),
                "wide",
                split_axis=0,
                concat_axis=1,
                tiled=True,
            )
            * sea_float[None]
        )
    return energy


def solution(mesh):
    return jax.shard_map(
        body,
        mesh=mesh,
        in_specs=(P("wide", "slab", None), P("slab", None), P(), P(), P()),
        out_specs=P("wide", "slab", None),
        check_vma=False,
    )
```

profile of v0, /device:TPU:0, one launch (start us, length us, event | category | flops | bytes accessed | tf_op | source)
XLA Modules:
  0.0 121.6 jit_solution(2893711885013228222)
XLA Ops:
  0.0 0.8 convert_element_type.19
  0.8 1.2 copy_multiply_fusion
  2.1 2.4 %collective-permute-start = (f32[144,1,128]{2,0,1:T(8,128)S(1)}, f32[144,1,128]{2,0,1:T(8,128)S(1)}, u32[]{:S(2)}, u32[]{:S(2)}) collective-permute-start(f32[144,1,128]{2,0,1:T(8,128)S(1)} %get-tuple-element.17), channel_id=1, source_target_pairs={{0,8},{8,16},{16,24},{1,9},{9,17},{17,25},{2,10},{10,18},{18,26},{... | collective-permute-start | bytes 221192 | tf_op jit(solution)/shard_map/ppermute | solution.py:23
  4.5 1.3 %collective-permute-start.1 = (f32[144,1,128]{2,0,1:T(8,128)S(1)}, f32[144,1,128]{2,0,1:T(8,128)S(1)}, u32[]{:S(2)}, u32[]{:S(2)}) collective-permute-start(f32[144,1,128]{2,0,1:T(8,128)S(1)} %get-tuple-element.18), channel_id=1, source_target_pairs={{8,0},{16,8},{24,16},{9,1},{17,9},{25,17},{10,2},{18,10},{26,18},{... | collective-permute-start | bytes 221192 | tf_op jit(solution)/shard_map/ppermute | solution.py:25
  5.8 1.2 fusion.26
  7.0 1.2 fusion.27
  8.1 0.6 compare_and_fusion
  8.7 0.6 compare_select_fusion
  9.4 0.1 select_reduce_fusion
  9.5 0.1 abs_subtract_fusion
  9.6 0.6 broadcast_maximum_fusion.1
  10.3 0.7 pad_clamp_fusion
  11.0 5.1 %gather_fusion = bf16[1152,1152]{1,0:T(8,128)(2,1)} fusion(bf16[1152,1152]{1,0:T(8,128)(2,1)S(1)} %copy-done, s32[2048]{0:T(1024)S(1)} %pad_clamp_fusion), kind=kCustom, calls=%fused_computation | custom fusion | bytes 5313024 | tf_op jit(solution)/shard_map/jit(_take)/gather | solution.py:77
  16.1 2.9 %fusion.11 = f32[144,8,128]{2,0,1:T(8,128)} fusion(f32[144,1,128]{2,0,1:T(8,128)S(1)} %collective-permute-done.1, f32[144,8,128]{2,0,1:T(8,128)S(1)} %copy_multiply_fusion, f32[144,1,128]{2,0,1:T(8,128)S(1)} %collective-permute-done, f32[144,8,127]{2,0,1:T(8,128)} %get-tuple-element.14, f32[144,8,1]{2,0,1:T(8,128)} %get-tuple-element.16, ...), kind=kLoop, calls=%fused_computation.22 | loop fusion | flops 1916928 | bytes 2509632 | tf_op jit(solution)/shard_map/add | solution.py:49
  19.0 6.6 %all-to-all-start = ((f32[144,8,128]{2,0,1:T(8,128)}), f32[144,8,128]{2,0,1:T(8,128)S(1)}, u32[]{:S(2)}, u32[]{:S(2)}) async-start(f32[144,8,128]{2,0,1:T(8,128)} %fusion.11), calls=%async_computation | async-start | bytes 1179648 | tf_op jit(solution)/shard_map/all_to_all | solution.py:87
  25.7 3.6 %broadcast_select_fusion = bf16[1152,1152]{1,0:T(8,128)(2,1)} fusion(bf16[1152,1152]{1,0:T(8,128)(2,1)} %gather_fusion, pred[1152]{0:T(1024)(128)(4,1)S(1)} %copy-done.7), kind=kLoop, calls=%fused_computation.2 | loop fusion | flops 1327104 | bytes 5309568 | tf_op jit(solution)/shard_map/jit(_take)/select_n | solution.py:77
  29.3 5.2 %copy.17 = bf16[1152,1152]{0,1:T(8,128)(2,1)} copy(bf16[1152,1152]{1,0:T(8,128)(2,1)} %broadcast_select_fusion) | data formatting | bytes 5308416 | tf_op jit(solution)/shard_map/jit(_take)/select_n | solution.py:77
  34.6 9.2 %gather_fusion.1 = bf16[1152,1152]{1,0:T(8,128)(2,1)} fusion(bf16[1152,1152]{0,1:T(8,128)(2,1)} %copy.17, s32[2048]{0:T(1024)S(1)} %pad_clamp_fusion), kind=kCustom, calls=%fused_computation.1 | custom fusion | bytes 5313024 | tf_op jit(solution)/shard_map/jit(_take)/gather | solution.py:77
  43.8 3.1 %convolution_multiply_fusion.1 = f32[1152,128]{1,0:T(8,128)S(1)} fusion(f32[1152,128]{1,0:T(8,128)S(1)} %bitcast.38, bf16[1152,128]{1,0:T(8,128)(2,1)S(1)} %bitcast_convert_fusion.1, bf16[1152,1152]{1,0:T(8,128)(2,1)} %gather_fusion.1, pred[1152]{0:T(1024)(128)(4,1)S(1)} %copy-done.7), kind=kOutput, calls=%fused_computation.13 | convolution fusion | flops 341213184 | bytes 4129920 | tf_op jit(solution)/shard_map/dot_general | solution.py:65
  47.0 1.0 fusion.5
  48.0 22.8 %all_to_all.66 = f32[1152,1,128]{2,1,0:T(1,128)S(1)} all-to-all(f32[1152,1,128]{2,1,0:T(1,128)S(1)} %bitcast.45), channel_id=1, replica_groups=mesh['slab'=4,'wide'=8] {'wide'}, dimensions={0} | all-to-all | bytes 1179648 | tf_op jit(solution)/shard_map/all_to_all | solution.py:85
  70.9 0.2 fusion.24
  71.1 2.6 %collective-permute-start.2 = (f32[144,1,128]{2,0,1:T(8,128)S(1)}, f32[144,1,128]{2,0,1:T(8,128)S(1)}, u32[]{:S(2)}, u32[]{:S(2)}) collective-permute-start(f32[144,1,128]{2,0,1:T(8,128)S(1)} %get-tuple-element.11), channel_id=1, source_target_pairs={{0,8},{8,16},{16,24},{1,9},{9,17},{17,25},{2,10},{10,18},{18,26},{... | collective-permute-start | bytes 221192 | tf_op jit(solution)/shard_map/ppermute | solution.py:23
  73.8 1.3 %collective-permute-start.3 = (f32[144,1,128]{2,0,1:T(8,128)S(1)}, f32[144,1,128]{2,0,1:T(8,128)S(1)}, u32[]{:S(2)}, u32[]{:S(2)}) collective-permute-start(f32[144,1,128]{2,0,1:T(8,128)S(1)} %get-tuple-element.12), channel_id=1, source_target_pairs={{8,0},{16,8},{24,16},{9,1},{17,9},{25,17},{10,2},{18,10},{26,18},{... | collective-permute-start | bytes 221192 | tf_op jit(solution)/shard_map/ppermute | solution.py:25
  75.1 0.2 fusion.23
  75.3 2.4 %collective-permute-done.3 = f32[144,1,128]{2,0,1:T(8,128)S(1)} collective-permute-done((f32[144,1,128]{2,0,1:T(8,128)S(1)}, f32[144,1,128]{2,0,1:T(8,128)S(1)}, u32[]{:S(2)}, u32[]{:S(2)}) %collective-permute-start.3) | collective-permute-done | bytes 73760 | tf_op jit(solution)/shard_map/ppermute | solution.py:25
  77.8 0.5 fusion.7
  78.3 19.3 %all_to_all.67 = f32[144,8,128]{2,0,1:T(8,128)S(1)} all-to-all(f32[144,8,128]{2,0,1:T(8,128)S(1)} %fusion.7), channel_id=1, replica_groups=mesh['slab'=4,'wide'=8] {'wide'}, dimensions={1} | all-to-all | bytes 1179648 | tf_op jit(solution)/shard_map/all_to_all | solution.py:87
  97.6 1.2 convolution_multiply_fusion
  98.8 1.0 fusion.2
  99.8 20.8 %all_to_all.68 = f32[1152,1,128]{2,1,0:T(1,128)S(1)} all-to-all(f32[1152,1,128]{2,1,0:T(1,128)S(1)} %bitcast.44), channel_id=1, replica_groups=mesh['slab'=4,'wide'=8] {'wide'}, dimensions={0} | all-to-all | bytes 1179648 | tf_op jit(solution)/shard_map/all_to_all | solution.py:85
  120.6 1.0 copy.20
  (31 shorter events, 0.4 us)
Async XLA Ops:
  0.0 11.0 %copy-start = (bf16[1152,1152]{1,0:T(8,128)(2,1)S(1)}, bf16[1152,1152]{1,0:T(8,128)(2,1)}, u32[]{:S(2)}) copy-start(bf16[1152,1152]{1,0:T(8,128)(2,1)} %param.9) | copy-start | bytes 7962628
  2.0 6.1 %copy-start.2 = (s32[1152]{0:T(1024)S(1)}, s32[1152]{0:T(1024)}, u32[]{:S(2)}) copy-start(s32[1152]{0:T(1024)} %param.8) | copy-start | bytes 13828
  2.0 7.4 %copy-start.8 = (f32[32]{0:T(128)S(1)}, f32[32]{0:T(128)}, u32[]{:S(2)}) copy-start(f32[32]{0:T(128)} %param.7) | copy-start | bytes 388
  2.1 14.0 %collective-permute-start = (f32[144,1,128]{2,0,1:T(8,128)S(1)}, f32[144,1,128]{2,0,1:T(8,128)S(1)}, u32[]{:S(2)}, u32[]{:S(2)}) collective-permute-start(f32[144,1,128]{2,0,1:T(8,128)S(1)} %get-tuple-element.17), channel_id=1, source_target_pairs={{0,8},{8,16},{16,24},{1,9},{9,17},{17,25},{2,10},{10,18},{18,26},{... | collective-permute-start | bytes 221192 | tf_op jit(solution)/shard_map/ppermute | solution.py:23
  4.5 11.6 %collective-permute-start.1 = (f32[144,1,128]{2,0,1:T(8,128)S(1)}, f32[144,1,128]{2,0,1:T(8,128)S(1)}, u32[]{:S(2)}, u32[]{:S(2)}) collective-permute-start(f32[144,1,128]{2,0,1:T(8,128)S(1)} %get-tuple-element.18), channel_id=1, source_target_pairs={{8,0},{16,8},{24,16},{9,1},{17,9},{25,17},{10,2},{18,10},{26,18},{... | collective-permute-start | bytes 221192 | tf_op jit(solution)/shard_map/ppermute | solution.py:25
  16.1 9.6 %copy-start.7 = (pred[1152]{0:T(1024)(128)(4,1)S(1)}, pred[1152]{0:T(1024)(128)(4,1)}, u32[]{:S(2)}) copy-start(pred[1152]{0:T(1024)(128)(4,1)} %compare_and_fusion) | copy-start | bytes 3460
  19.0 24.8 %all-to-all-start = ((f32[144,8,128]{2,0,1:T(8,128)}), f32[144,8,128]{2,0,1:T(8,128)S(1)}, u32[]{:S(2)}, u32[]{:S(2)}) async-start(f32[144,8,128]{2,0,1:T(8,128)} %fusion.11), calls=%async_computation | async-start | bytes 1179648 | tf_op jit(solution)/shard_map/all_to_all | solution.py:87
  43.8 3.2 %copy-start.1 = (bf16[1152,1152]{1,0:T(8,128)(2,1)S(1)}, bf16[1152,1152]{1,0:T(8,128)(2,1)}, u32[]{:S(2)}) copy-start(bf16[1152,1152]{1,0:T(8,128)(2,1)} %gather_fusion.1) | copy-start | bytes 7962628
  70.9 6.9 %copy-start.3 = (f32[144]{0:T(256)S(1)}, f32[144]{0:T(256)}, u32[]{:S(2)}) copy-start(f32[144]{0:T(256)} %get-tuple-element.19) | copy-start | bytes 1732
  70.9 6.9 %copy-start.4 = (f32[144]{0:T(256)S(1)}, f32[144]{0:T(256)}, u32[]{:S(2)}) copy-start(f32[144]{0:T(256)} %get-tuple-element.20) | copy-start | bytes 1732
  70.9 6.9 %copy-start.5 = (f32[144]{0:T(256)S(1)}, f32[144]{0:T(256)}, u32[]{:S(2)}) copy-start(f32[144]{0:T(256)} %get-tuple-element.21) | copy-start | bytes 1732
  70.9 6.9 %copy-start.6 = (f32[144]{0:T(256)S(1)}, f32[144]{0:T(256)}, u32[]{:S(2)}) copy-start(f32[144]{0:T(256)} %get-tuple-element.22) | copy-start | bytes 1732
  71.1 4.2 %collective-permute-start.2 = (f32[144,1,128]{2,0,1:T(8,128)S(1)}, f32[144,1,128]{2,0,1:T(8,128)S(1)}, u32[]{:S(2)}, u32[]{:S(2)}) collective-permute-start(f32[144,1,128]{2,0,1:T(8,128)S(1)} %get-tuple-element.11), channel_id=1, source_target_pairs={{0,8},{8,16},{16,24},{1,9},{9,17},{17,25},{2,10},{10,18},{18,26},{... | collective-permute-start | bytes 221192 | tf_op jit(solution)/shard_map/ppermute | solution.py:23
  73.8 4.0 %collective-permute-start.3 = (f32[144,1,128]{2,0,1:T(8,128)S(1)}, f32[144,1,128]{2,0,1:T(8,128)S(1)}, u32[]{:S(2)}, u32[]{:S(2)}) collective-permute-start(f32[144,1,128]{2,0,1:T(8,128)S(1)} %get-tuple-element.12), channel_id=1, source_target_pairs={{8,0},{16,8},{24,16},{9,1},{17,9},{25,17},{10,2},{18,10},{26,18},{... | collective-permute-start | bytes 221192 | tf_op jit(solution)/shard_map/ppermute | solution.py:25
where the time goes:
time: 122 us
  blocking collectives  62.9 us (52%)
  local copies, waits for them, and re-layouts  23.4 us (19%)
  starting transfers between devices  14.2 us (12%)
  other arithmetic  12.1 us (10%)
  matrix products  6.23 us (5%)
  waiting for transfers between devices  2.46 us (2%)
    all_to_all x2, blocking collectives, body(): lax.all_to_all(interact(lax.all_to_all(moved, 'wide', split_axis=1, conca...  43.6 us
    all_to_all x1, blocking collectives, body(): lax.all_to_all(moved, 'wide', split_axis=1, concat_axis=0, tiled=True)  19.3 us
    gather x1, local copies, waits for them, and re-layouts, body(): jnp.take(jnp.take(coupling, slot_owner, axis=0), slot_owner, axis=1)  9.24 us
    all_to_all x1, starting transfers between devices, body(): lax.all_to_all(moved, 'wide', split_axis=1, concat_axis=0, tiled=True)  6.62 us
    select_n x1, local copies, waits for them, and re-layouts, body(): jnp.take(coupling, slot_owner, axis=0)  5.25 us
    gather x1, local copies, waits for them, and re-layouts, body(): jnp.take(coupling, slot_owner, axis=0)  5.11 us
    ppermute x2, starting transfers between devices, extended(): lax.ppermute(tail, axis, [(i, (i + 1) % count) for i in range(ends)])  5.02 us
    dot_general x2, matrix products, interact(): jnp.dot(slot_table, rounded, preferred_element_type=jnp.float32)  4.31 us
  transfers between devices with their start and end apart: 5, of which 1 were waited for; matrix products, arithmetic and copies ran while one was open for 24% of the time, Pallas kernels for 0%

commit v1 on v0

--- a/solution.py
+++ b/solution.py
@@ -1,13 +1,18 @@
+import functools
 import math
 
 import jax
 import jax.numpy as jnp
+import numpy as np
 from jax import lax
+from jax.experimental import pallas as pl
+from jax.experimental.pallas import tpu as pltpu
 from jax.sharding import PartitionSpec as P
 
 ND = 36
 STEPS = 2
-
+LANES = 128
+SUBS = 8
 
 time_step = 0.5
 
@@ -70,7 +75,7 @@
     return updated.reshape(moved.shape)
 
 
-def body(spectrum, sea_mask, courant, slot_owner, coupling):
+def general_body(spectrum, sea_mask, courant, slot_owner, coupling):
     slot_count = spectrum.shape[0]
     wide_index = lax.axis_index("wide")
     sea_float = sea_mask.astype(jnp.float32)
@@ -97,7 +102,306 @@
     return energy
 
 
+def ring_order(count):
+    ring = list(range(0, count, 2)) + list(range(1, count, 2))[::-1]
+    place = [0] * count
+    for block, device in enumerate(ring):
+        place[device] = block
+    return place, ring
+
+
+def trig_table():
+    angle = np.arange(ND, dtype=np.float32) * np.float32(2.0 * math.pi / ND)
+    return np.cos(angle), np.sin(angle)
+
+
+def shares(east, north):
+    return (
+        1.0 - jnp.abs(east) - jnp.abs(north),
+        jnp.maximum(east, 0.0),
+        jnp.maximum(-east, 0.0),
+        jnp.maximum(north, 0.0),
+        jnp.maximum(-north, 0.0),
+    )
+
+
+def swap_lane_blocks(parts, width):
+    count = len(parts)
+    lane = lax.broadcasted_iota(jnp.int32, parts[0].shape, 1) // width
+    bit = 1
+    while bit < count:
+        low = (lane & bit) == 0
+        done = list(parts)
+        for a in range(count):
+            if a & bit:
+                continue
+            b = a | bit
+            done[a] = jnp.where(low, parts[a], pltpu.roll(parts[b], bit * width, 1))
+            done[b] = jnp.where(low, pltpu.roll(parts[a], LANES - bit * width, 1), parts[b])
+        parts = done
+        bit *= 2
+    return parts
+
+
+def lookup_columns(owner, courant, table):
+    lane = lax.broadcasted_iota(jnp.int32, (owner.shape[0], LANES), 1)
+    band = owner // ND
+    heading = owner - band * ND
+    speed = jnp.sum(jnp.where(lane == band, courant, 0.0), axis=1, keepdims=True)
+    cosine = jnp.sum(jnp.where(lane == heading, table[0:1], 0.0), axis=1, keepdims=True)
+    sine = jnp.sum(jnp.where(lane == heading, table[1:2], 0.0), axis=1, keepdims=True)
+    return speed * cosine, speed * sine
+
+
+def spread_kernel(place, cols, x_ref, sea_ref, prev_ref, next_ref, owner_ref, courant_ref, table_ref, out_ref):
+    slots = prev_ref.shape[0]
+    courant, table = courant_ref[...], table_ref[...]
+    sea = [jnp.broadcast_to(sea_ref[r : r + 1, :], (SUBS, LANES)) for r in range(SUBS)]
+
+    def group(g, carry):
+        base = pl.multiple_of(g * SUBS, SUBS)
+        here = pl.ds(base, SUBS)
+        east, north = lookup_columns(owner_ref[here, :], courant, table)
+        remain, west_in, east_in, south_in, north_in = shares(east, north)
+        rows = [
+            x_ref[pl.ds(base * SUBS + r, SUBS, stride=SUBS), :] * sea[r] for r in range(SUBS)
+        ]
+        rows = [prev_ref[here, :]] + rows + [next_ref[here, :]]
+        moved = []
+        for r in range(1, SUBS + 1):
+            value = remain * rows[r] + west_in * pltpu.roll(rows[r], 1, 1)
+            value = value + east_in * pltpu.roll(rows[r], LANES - 1, 1)
+            value = value + south_in * rows[r - 1]
+            moved.append(value + north_in * rows[r + 1])
+        blocks = swap_lane_blocks(moved, cols)
+        for device, block in enumerate(place):
+            out_ref[device, here, :] = blocks[block]
+        return carry
+
+    lax.fori_loop(0, slots // SUBS, group, 0)
+
+
+def gather_kernel(ring, cols, x_ref, out_ref):
+    slots = x_ref.shape[1]
+
+    def group(g, carry):
+        base = pl.multiple_of(g * SUBS, SUBS)
+        here = pl.ds(base, SUBS)
+        rows = swap_lane_blocks([x_ref[device, here, :] for device in ring], cols)
+        for r in range(SUBS):
+            out_ref[pl.ds(base * SUBS + r, SUBS, stride=SUBS), :] = rows[r]
+        return carry
+
+    lax.fori_loop(0, slots // SUBS, group, 0)
+
+
+def table_kernel(row_ref, col_ref, coupling_ref, courant_ref, table_ref, out_ref, share_ref, half_ref):
+    count = row_ref.shape[1]
+    owner = row_ref[...]
+    step = LANES
+    for c in range(0, count, step):
+        line = lax.broadcasted_iota(jnp.int32, (count, step), 0)
+        pick = (line == owner[:, c : c + step]).astype(jnp.bfloat16)
+        half_ref[:, c : c + step] = jnp.dot(
+            coupling_ref[...], pick, preferred_element_type=jnp.float32
+        ).astype(jnp.bfloat16)
+    for c in range(0, count, step):
+        line = lax.broadcasted_iota(jnp.int32, (step, count), 1)
+        pick = (line == col_ref[c : c + step, :]).astype(jnp.bfloat16)
+        out_ref[c : c + step, :] = jnp.dot(
+            pick, half_ref[...], preferred_element_type=jnp.float32
+        ).astype(jnp.bfloat16)
+    band = owner // ND
+    heading = owner - band * ND
+    line = lax.broadcasted_iota(jnp.int32, (LANES, count), 0)
+    speed = jnp.sum(jnp.where(line == band, courant_ref[...], 0.0), axis=0, keepdims=True)
+    cosine = jnp.sum(jnp.where(line == heading, table_ref[:, 0:1], 0.0), axis=0, keepdims=True)
+    sine = jnp.sum(jnp.where(line == heading, table_ref[:, 1:2], 0.0), axis=0, keepdims=True)
+    for k, share in enumerate(shares(speed * cosine, speed * sine)):
+        share_ref[k : k + 1, :] = share
+
+
+def contract(moved_ref, rounded_ref, square_ref, table_ref, sea, store):
+    count = moved_ref.shape[1]
+    step = LANES
+    for c in range(0, count, step):
+        gain = lax.dot_general(
+            rounded_ref[...],
+            table_ref[c : c + step, :],
+            (((1,), (1,)), ((), ())),
+            preferred_element_type=jnp.float32,
+        )
+        loss = jnp.dot(square_ref[...], table_ref[:, c : c + step], preferred_element_type=jnp.float32)
+        moved = moved_ref[:, c : c + step]
+        store(c, jnp.maximum(moved + time_step * (moved * gain - loss), 0.0) * sea)
+
+
+def first_kernel(cols, x_ref, table_ref, sea_ref, out_ref, n_ref, s_ref, w_ref, e_ref, moved_ref, rounded_ref, square_ref):
+    count, points = x_ref.shape
+    step = LANES
+    for c in range(0, count, step):
+        moved = x_ref[c : c + step, :].T
+        moved_ref[:, c : c + step] = moved
+        rounded_ref[:, c : c + step] = moved.astype(jnp.bfloat16)
+        square_ref[:, c : c + step] = (moved * moved).astype(jnp.bfloat16)
+
+    def store(c, value):
+        there = slice(c, c + step)
+        out_ref[:, there] = value
+        n_ref[:, there] = value[:cols]
+        s_ref[:, there] = value[points - cols :]
+        for r in range(points // cols):
+            w_ref[r : r + 1, there] = value[r * cols : r * cols + 1]
+            e_ref[r : r + 1, there] = value[(r + 1) * cols - 1 : (r + 1) * cols]
+
+    contract(moved_ref, rounded_ref, square_ref, table_ref, sea_ref[...], store)
+
+
+def second_kernel(cols, x_ref, n_ref, s_ref, w_ref, e_ref, share_ref, table_ref, sea_ref, out_ref, moved_ref, rounded_ref, square_ref):
+    points, count = x_ref.shape
+    step = LANES
+    line = lax.broadcasted_iota(jnp.int32, (points, step), 0) % cols
+    for c in range(0, count, step):
+        there = slice(c, c + step)
+        here = x_ref[:, there]
+        share = [share_ref[k : k + 1, there] for k in range(5)]
+
+        def along(ref):
+            return jnp.concatenate(
+                [jnp.broadcast_to(ref[r : r + 1, there], (cols, step)) for r in range(points // cols)], axis=0
+            )
+
+        west = jnp.where(line == 0, along(w_ref), pltpu.roll(here, 1, 0))
+        east = jnp.where(line == cols - 1, along(e_ref), pltpu.roll(here, points - 1, 0))
+        south = jnp.concatenate([s_ref[:, there], here[: points - cols]], axis=0)
+        north = jnp.concatenate([here[cols:], n_ref[:, there]], axis=0)
+        moved = share[0] * here + share[1] * west
+        moved = moved + share[2] * east
+        moved = moved + share[3] * south
+        moved = moved + share[4] * north
+        moved_ref[:, there] = moved
+        rounded_ref[:, there] = moved.astype(jnp.bfloat16)
+        square_ref[:, there] = (moved * moved).astype(jnp.bfloat16)
+
+    def store(c, value):
+        out_ref[c : c + step, :] = value.T
+
+    contract(moved_ref, rounded_ref, square_ref, table_ref, sea_ref[...], store)
+
+
+def block_body(spectrum, sea_mask, courant, slot_owner, coupling):
+    slots, rows, lons = spectrum.shape
+    wide, slabs = lax.axis_size("wide"), lax.axis_size("slab")
+    count = slots * wide
+    cols = lons // wide
+    points = rows * cols
+    wide_index = lax.axis_index("wide")
+    place, ring = ring_order(wide)
+    vmem = pl.BlockSpec(memory_space=pltpu.VMEM)
+    f32 = jnp.float32
+
+    def call(kernel, name, outs, n_in, scratch=(), flops=0):
+        return pl.pallas_call(
+            kernel,
+            out_shape=outs,
+            in_specs=[vmem] * n_in,
+            out_specs=jax.tree.map(lambda _: vmem, outs),
+            scratch_shapes=scratch,
+            cost_estimate=pl.CostEstimate(flops=flops, transcendentals=0, bytes_accessed=0),
+            name=name,
+        )
+
+    shape = jax.ShapeDtypeStruct
+    sea = sea_mask.astype(f32)
+    first_row = spectrum[:, 0, :] * sea[0]
+    last_row = spectrum[:, rows - 1, :] * sea[rows - 1]
+    prev_row = lax.ppermute(last_row, "slab", [(i, i + 1) for i in range(slabs - 1)])
+    next_row = lax.ppermute(first_row, "slab", [(i + 1, i) for i in range(slabs - 1)])
+    own = lax.dynamic_slice_in_dim(slot_owner, wide_index * slots, slots, 0)
+    cosine, sine = trig_table()
+    table = np.zeros((SUBS, LANES), np.float32)
+    table[0, :ND], table[1, :ND] = cosine, sine
+    speeds = jnp.pad(courant, (0, LANES - courant.shape[0]))
+
+    blocks = call(
+        functools.partial(spread_kernel, place, cols),
+        "spread",
+        shape((wide, slots, LANES), f32),
+        7,
+    )(spectrum.reshape(slots * rows, lons), sea, prev_row, next_row, own[:, None], speeds[None, :], jnp.asarray(table))
+    arrived = lax.all_to_all(blocks, "wide", 0, 0).reshape(count, points)
+
+    slot_table, share = call(
+        table_kernel,
+        "table",
+        (shape((count, count), jnp.bfloat16), shape((SUBS, count), f32)),
+        5,
+        (pltpu.VMEM((count, count), jnp.bfloat16),),
+        flops=4 * count**3,
+    )(slot_owner[None, :], slot_owner[:, None], coupling, speeds[:, None], jnp.asarray(table.T))
+
+    block_index = jnp.asarray(place, jnp.int32)[wide_index]
+    sea_block = lax.dynamic_slice_in_dim(sea, block_index * cols, cols, 1).reshape(points, 1)
+
+    scratch = (
+        pltpu.VMEM((points, count), f32),
+        pltpu.VMEM((points, count), jnp.bfloat16),
+        pltpu.VMEM((points, count), jnp.bfloat16),
+    )
+    energy, first, last, west, east = call(
+        functools.partial(first_kernel, cols),
+        "first",
+        (
+            shape((points, count), f32),
+            shape((cols, count), f32),
+            shape((cols, count), f32),
+            shape((rows, count), f32),
+            shape((rows, count), f32),
+        ),
+        3,
+        scratch,
+        flops=4 * points * count**2,
+    )(arrived, slot_table, sea_block)
+
+    both = ("slab", "wide")
+    down = [(s * wide + w, (s + 1) * wide + w) for s in range(slabs - 1) for w in range(wide)]
+    up = [(b, a) for a, b in down]
+    right = [
+        (s * wide + ring[j], s * wide + ring[(j + 1) % wide]) for s in range(slabs) for j in range(wide)
+    ]
+    left = [(b, a) for a, b in right]
+    from_south = lax.ppermute(last, both, down)
+    from_north = lax.ppermute(first, both, up)
+    from_west = lax.ppermute(east, both, right)
+    from_east = lax.ppermute(west, both, left)
+
+    updated = call(
+        functools.partial(second_kernel, cols),
+        "second",
+        shape((count, points), f32),
+        8,
+        scratch,
+        flops=4 * points * count**2,
+    )(energy, from_north, from_south, from_west, from_east, share, slot_table, sea_block)
+    back = lax.all_to_all(updated.reshape(wide, slots, points), "wide", 0, 0)
+    evolved = call(
+        functools.partial(gather_kernel, ring, cols),
+        "gather",
+        shape((slots * rows, lons), f32),
+        1,
+    )(back)
+    return evolved.reshape(slots, rows, lons)
+
+
 def solution(mesh):
+    wide, slabs = mesh.shape["wide"], mesh.shape["slab"]
+
+    def body(spectrum, *rest):
+        slots, rows, lons = spectrum.shape
+        fits = rows == SUBS and lons == LANES and wide == SUBS and slots % SUBS == 0
+        fits = fits and (slots * wide) % LANES == 0
+        return (block_body if fits else general_body)(spectrum, *rest)
+
     return jax.shard_map(
         body,
         mesh=mesh,

time: 122 us -> 96 us (0.79)
  blocking collectives: 62.9 us -> 21.6 us
  Pallas kernels: 0 us -> 38.4 us
  local copies, waits for them, and re-layouts: 23.4 us -> 10.8 us
  other arithmetic: 12.1 us -> 0.73 us
  matrix products: 6.23 us -> 0 us
  starting transfers between devices: 14.2 us -> 18.1 us
  waiting for transfers between devices: 2.46 us -> 5.1 us
    all_to_all x3 -> x1, blocking collectives: 62.9 us -> 21.6 us  [block_body(): back = lax.all_to_all(updated.reshape(wide, slots, points), 'wide', 0, 0)]
    pallas_call x0 -> x5, Pallas kernels: none -> 38.4 us  [the longest x1 14.3 us: block_body(): call(table_kernel, 'table', (shape((count, count), jnp.bfloat16), shape((...]
    gather x2 -> x0, local copies, waits for them, and re-layouts: 14.3 us -> none  [the longest x1 9.24 us: body(): jnp.take(jnp.take(coupling, slot_owner, axis=0), slot_owner, axis=1)]
    dot_general x4 -> x0, matrix products: 6.23 us -> none  [the longest x2 4.31 us: interact(): jnp.dot(slot_table, rounded, preferred_element_type=jnp.float32)]
    select_n x1 -> x0, local copies, waits for them, and re-layouts: 5.25 us -> none  [body(): jnp.take(coupling, slot_owner, axis=0)]
    ppermute x4 -> x6, starting transfers between devices: 7.61 us -> 12.3 us  [the longest x1 5.26 us: block_body(): from_south = lax.ppermute(last, both, down)]
    broadcast_in_dim x0 -> x5, local copies, waits for them, and re-layouts: none -> 4.35 us  [the longest x2 1.96 us: block_body(): speeds[:, None]]
    select_n x3 -> x0, other arithmetic: 4.32 us -> none  [the longest x1 3.64 us: body(): jnp.take(coupling, slot_owner, axis=0)]
  transfers between devices with their start and end apart: 5 -> 7, of which waited for: 1 -> 3; matrix products, arithmetic and copies ran while one was open for 24% -> 8% of each run, Pallas kernels for 0% -> 15%
where the time goes in v1:
time: 96 us; the launch traced here: 95.4 us
  Pallas kernels  38.4 us (40%)
  blocking collectives  21.6 us (22%)
  starting transfers between devices  18.1 us (19%)
  local copies, waits for them, and re-layouts  10.8 us (11%)
  waiting for transfers between devices  5.1 us (5%)
    all_to_all x1, blocking collectives, block_body(): back = lax.all_to_all(updated.reshape(wide, slots, points), 'wide', 0, 0)  21.6 us
    pallas_call x1, Pallas kernels, block_body(): call(table_kernel, 'table', (shape((count, count), jnp.bfloat16), shape((...  14.3 us
    pallas_call x1, Pallas kernels, block_body(): call(functools.partial(spread_kernel, place, cols), 'spread', shape((wide...  8.84 us
    pallas_call x1, Pallas kernels, block_body(): call(functools.partial(gather_kernel, ring, cols), 'gather', shape((slots...  5.82 us
    all_to_all x1, starting transfers between devices, block_body(): arrived = lax.all_to_all(blocks, 'wide', 0, 0).reshape(count, points)  5.81 us
    ppermute x1, starting transfers between devices, block_body(): from_south = lax.ppermute(last, both, down)  5.26 us
    pallas_call x1, Pallas kernels, block_body(): call(functools.partial(second_kernel, cols), 'second', shape((count, poin...  4.87 us
    pallas_call x1, Pallas kernels, block_body(): call(functools.partial(first_kernel, cols), 'first', (shape((points, coun...  4.53 us
  transfers between devices with their start and end apart: 7, of which 3 were waited for; matrix products, arithmetic and copies ran while one was open for 8% of the time, Pallas kernels for 15%

profile of v1, /device:TPU:0, one launch (start us, length us, event | category | flops | bytes accessed | tf_op | source)
XLA Modules:
  0.0 95.4 jit_solution(7838726010894023326)
XLA Ops:
  0.0 0.7 convert_element_type.5.sea_ref
  0.7 1.5 %fusion = (f32[144,1,128]{2,1,0:T(1,128)S(1)}, f32[144,1,128]{2,1,0:T(1,128)S(1)}) fusion(f32[144,8,128]{2,1,0:T(8,128)} %param.8), kind=kLoop, calls=%fused_computation.7 | loop fusion | bytes 294912 | tf_op jit(solution)/shard_map/slice | solution.py:316
  2.2 2.4 %collective-permute-start = (f32[144,128]{1,0:T(8,128)S(1)}, f32[144,128]{1,0:T(8,128)S(1)}, u32[]{:S(2)}, u32[]{:S(2)}) collective-permute-start(f32[144,128]{1,0:T(8,128)S(1)} %broadcast_multiply_fusion.1), channel_id=1, source_target_pairs={{0,8},{8,16},{16,24},{1,9},{9,17},{17,25},{2,10},{10,18},{18,26},{... | collective-permute-start | bytes 221192 | tf_op jit(solution)/shard_map/ppermute | solution.py:318
  4.7 1.3 %collective-permute-start.1 = (f32[144,128]{1,0:T(8,128)S(1)}, f32[144,128]{1,0:T(8,128)S(1)}, u32[]{:S(2)}, u32[]{:S(2)}) collective-permute-start(f32[144,128]{1,0:T(8,128)S(1)} %broadcast_multiply_fusion), channel_id=1, source_target_pairs={{8,0},{16,8},{24,16},{9,1},{17,9},{25,17},{10,2},{18,10},{26,18},{... | collective-permute-start | bytes 221192 | tf_op jit(solution)/shard_map/ppermute | solution.py:319
  6.0 0.8 dynamic_slice.9
  6.7 0.8 copy.16.owner_ref
  7.5 1.2 %pad_bitcast_fusion = (f32[128,1]{0,1:T(1,128)S(1)}, f32[1,128]{1,0:T(1,128)}) fusion(f32[32]{0:T(128)} %param.10), kind=kLoop, calls=%fused_computation.4 | loop fusion | bytes 1152 | tf_op jit(solution)/shard_map/broadcast_in_dim | solution.py:341
  8.7 1.2 %collective-permute-done.1.next_ref = f32[144,128]{1,0:T(8,128)S(1)} collective-permute-done((f32[144,128]{1,0:T(8,128)S(1)}, f32[144,128]{1,0:T(8,128)S(1)}, u32[]{:S(2)}, u32[]{:S(2)}) %collective-permute-start.1) | collective-permute-done | bytes 73760 | tf_op jit(solution)/shard_map/ppermute | solution.py:319
  9.9 0.6 copy-done.2
  10.6 8.8 %spread.1 = f32[8,144,128]{2,1,0:T(8,128)} custom-call(f32[1152,128]{1,0:T(8,128)} %bitcast.22, f32[8,128]{1,0:T(8,128)} %copy-done.5, f32[144,128]{1,0:T(8,128)} %copy-done.1, f32[144,128]{1,0:T(8,128)} %copy-done.2, s32[144,1]{1,0:T(8,128)} %copy.16.owner_ref, f32[1,128]{1,0:T(1,128)} %get-tuple-element.24.courant_ref, f32[8,128]{1,0:T(8,128)} %constant.25.clone.table_ref), custom_call_target="tpu_custom_call" | custom-call | tf_op jit(solution)/shard_map/spread/pallas_call | solution.py:326
  19.4 5.8 %all-to-all-start = ((f32[8,144,128]{2,1,0:T(8,128)}), f32[8,144,128]{2,1,0:T(8,128)S(1)}, u32[]{:S(2)}, u32[]{:S(2)}) async-start(f32[8,144,128]{2,1,0:T(8,128)} %spread.1), calls=%async_computation | async-start | bytes 1179648 | tf_op jit(solution)/shard_map/all_to_all | solution.py:332
  25.2 0.6 broadcast_in_dim.17.row_ref
  25.8 1.0 %broadcast_in_dim.20.col_ref = s32[1152,1]{1,0:T(8,128)} reshape(s32[1152]{0:T(1024)S(1)} %copy-done.6) | data formatting | bytes 9216 | tf_op jit(solution)/shard_map/broadcast_in_dim | solution.py:341
  26.9 0.6 dynamic_slice.10
  28.0 0.8 constant_dynamic-slice_fusion
  28.8 0.7 reshape.22.sea_ref
  29.5 0.7 copy.18.courant_ref
  30.2 14.3 %table.1 = (bf16[1152,1152]{1,0:T(8,128)(2,1)}, f32[8,1152]{1,0:T(8,128)}) custom-call(s32[1,1152]{1,0:T(1,128)} %broadcast_in_dim.17.row_ref, s32[1152,1]{1,0:T(8,128)} %broadcast_in_dim.20.col_ref, bf16[1152,1152]{1,0:T(8,128)(2,1)} %coupling_ref.1, f32[128,1]{1,0:T(8,128)} %copy.18.courant_ref, f32[128,8]{1,0:T(8,128)} %constant.26.clone.table_ref), custom_call_target="tpu_custom_call" | custom-call | flops 6115295232 | tf_op jit(solution)/shard_map/table/pallas_call | solution.py:334
  44.5 0.8 copy-done
  45.3 4.5 %first.1 = (f32[128,1152]{1,0:T(8,128)}, f32[16,1152]{1,0:T(8,128)}, f32[16,1152]{1,0:T(8,128)}, f32[8,1152]{1,0:T(8,128)}, f32[8,1152]{1,0:T(8,128)}) custom-call(f32[1152,128]{1,0:T(8,128)} %bitcast.21, bf16[1152,1152]{1,0:T(8,128)(2,1)} %get-tuple-element.12.table_ref, f32[128,1]{1,0:T(8,128)} %reshape.22.sea_ref), custom_call_target="tpu_custom_call" | custom-call | flops 679477248 | tf_op jit(solution)/shard_map/first/pallas_call | solution.py:351
  49.9 1.3 %collective-permute-start.2 = (f32[16,1152]{1,0:T(8,128)}, f32[16,1152]{1,0:T(8,128)S(1)}, u32[]{:S(2)}, u32[]{:S(2)}) collective-permute-start(f32[16,1152]{1,0:T(8,128)} %get-tuple-element.14), channel_id=1, source_target_pairs={{8,0},{9,1},{10,2},{11,3},{12,4},{13,5},{14,6},{15,7},{16,8},{17,9... | collective-permute-start | bytes 221192 | tf_op jit(solution)/shard_map/ppermute | solution.py:374
  51.2 5.3 %collective-permute-start.3 = (f32[16,1152]{1,0:T(8,128)}, f32[16,1152]{1,0:T(8,128)S(1)}, u32[]{:S(2)}, u32[]{:S(2)}) collective-permute-start(f32[16,1152]{1,0:T(8,128)} %get-tuple-element.15), channel_id=1, source_target_pairs={{0,8},{1,9},{2,10},{3,11},{4,12},{5,13},{6,14},{7,15},{8,16},{9,17... | collective-permute-start | bytes 221192 | tf_op jit(solution)/shard_map/ppermute | solution.py:373
  56.4 1.8 %collective-permute-start.4 = (f32[8,1152]{1,0:T(8,128)}, f32[8,1152]{1,0:T(8,128)S(1)}, u32[]{:S(2)}, u32[]{:S(2)}) collective-permute-start(f32[8,1152]{1,0:T(8,128)} %get-tuple-element.16), channel_id=1, source_target_pairs={{0,2},{2,4},{4,6},{6,7},{7,5},{5,3},{3,1},{1,0},{8,10},{10,12},{12... | collective-permute-start | bytes 110600 | tf_op jit(solution)/shard_map/ppermute | solution.py:375
  58.2 0.3 collective-permute-start.5
  58.5 2.1 %collective-permute-done.4.w_ref = f32[8,1152]{1,0:T(8,128)S(1)} collective-permute-done((f32[8,1152]{1,0:T(8,128)}, f32[8,1152]{1,0:T(8,128)S(1)}, u32[]{:S(2)}, u32[]{:S(2)}) %collective-permute-start.4) | collective-permute-done | bytes 36896 | tf_op jit(solution)/shard_map/ppermute | solution.py:375
  60.6 1.7 %collective-permute-done.5.e_ref = f32[8,1152]{1,0:T(8,128)S(1)} collective-permute-done((f32[8,1152]{1,0:T(8,128)}, f32[8,1152]{1,0:T(8,128)S(1)}, u32[]{:S(2)}, u32[]{:S(2)}) %collective-permute-start.5) | collective-permute-done | bytes 36896 | tf_op jit(solution)/shard_map/ppermute | solution.py:376
  62.4 0.6 copy-done.8
  63.0 0.0 copy-done.3
  63.0 0.0 copy-done.4
  63.1 4.9 %second.1 = f32[1152,128]{1,0:T(8,128)} custom-call(f32[128,1152]{1,0:T(8,128)} %get-tuple-element.13.x_ref, f32[16,1152]{1,0:T(8,128)} %copy-done.3, f32[16,1152]{1,0:T(8,128)} %copy-done.4, f32[8,1152]{1,0:T(8,128)} %copy-done.7, f32[8,1152]{1,0:T(8,128)} %copy-done.8, f32[8,1152]{1,0:T(8,128)} %get-tuple-element.18.share_ref, ...), custom_call_target="tpu_custom_call" | custom-call | flops 679477248 | tf_op jit(solution)/shard_map/second/pallas_call | solution.py:378
  67.9 21.6 %all_to_all.10.x_ref = f32[8,144,128]{2,1,0:T(8,128)} all-to-all(f32[8,144,128]{2,1,0:T(8,128)} %bitcast.20), channel_id=1, replica_groups=mesh['slab'=4,'wide'=8] {'wide'}, dimensions={0} | all-to-all | bytes 1179648 | tf_op jit(solution)/shard_map/all_to_all | solution.py:386
  89.6 5.8 %gather.1 = f32[1152,128]{1,0:T(8,128)} custom-call(f32[8,144,128]{2,1,0:T(8,128)} %all_to_all.10.x_ref), custom_call_target="tpu_custom_call" | custom-call | tf_op jit(solution)/shard_map/gather/pallas_call | solution.py:387
  (22 shorter events, 0.1 us)
Async XLA Ops:
  0.0 26.8 %copy-start.9 = (s32[8]{0:T(128)S(1)}, s32[8]{0:T(128)}, u32[]{:S(2)}) copy-start(s32[8]{0:T(128)} %constant.27.clone) | copy-start | bytes 100
  0.0 25.2 %copy-start.6 = (s32[1152]{0:T(1024)S(1)}, s32[1152]{0:T(1024)}, u32[]{:S(2)}) copy-start(s32[1152]{0:T(1024)} %param.11) | copy-start | bytes 13828
  0.7 9.2 %copy-start.5 = (f32[8,128]{1,0:T(8,128)}, f32[8,128]{1,0:T(8,128)S(1)}, u32[]{:S(2)}) copy-start(f32[8,128]{1,0:T(8,128)S(1)} %convert_element_type.5.sea_ref) | copy-start | bytes 12292
  2.2 6.5 %collective-permute-start = (f32[144,128]{1,0:T(8,128)S(1)}, f32[144,128]{1,0:T(8,128)S(1)}, u32[]{:S(2)}, u32[]{:S(2)}) collective-permute-start(f32[144,128]{1,0:T(8,128)S(1)} %broadcast_multiply_fusion.1), channel_id=1, source_target_pairs={{0,8},{8,16},{16,24},{1,9},{9,17},{17,25},{2,10},{10,18},{18,26},{... | collective-permute-start | bytes 221192 | tf_op jit(solution)/shard_map/ppermute | solution.py:318
  4.7 5.3 %collective-permute-start.1 = (f32[144,128]{1,0:T(8,128)S(1)}, f32[144,128]{1,0:T(8,128)S(1)}, u32[]{:S(2)}, u32[]{:S(2)}) collective-permute-start(f32[144,128]{1,0:T(8,128)S(1)} %broadcast_multiply_fusion), channel_id=1, source_target_pairs={{8,0},{16,8},{24,16},{9,1},{17,9},{25,17},{10,2},{18,10},{26,18},{... | collective-permute-start | bytes 221192 | tf_op jit(solution)/shard_map/ppermute | solution.py:319
  8.7 1.2 %copy-start.1 = (f32[144,128]{1,0:T(8,128)}, f32[144,128]{1,0:T(8,128)S(1)}, u32[]{:S(2)}) copy-start(f32[144,128]{1,0:T(8,128)S(1)} %collective-permute-done.prev_ref) | copy-start | bytes 221188
  9.9 0.6 copy-start.2
  19.4 25.1 %all-to-all-start = ((f32[8,144,128]{2,1,0:T(8,128)}), f32[8,144,128]{2,1,0:T(8,128)S(1)}, u32[]{:S(2)}, u32[]{:S(2)}) async-start(f32[8,144,128]{2,1,0:T(8,128)} %spread.1), calls=%async_computation | async-start | bytes 1179648 | tf_op jit(solution)/shard_map/all_to_all | solution.py:332
  44.5 0.8 copy-start
  49.9 12.5 %collective-permute-start.2 = (f32[16,1152]{1,0:T(8,128)}, f32[16,1152]{1,0:T(8,128)S(1)}, u32[]{:S(2)}, u32[]{:S(2)}) collective-permute-start(f32[16,1152]{1,0:T(8,128)} %get-tuple-element.14), channel_id=1, source_target_pairs={{8,0},{9,1},{10,2},{11,3},{12,4},{13,5},{14,6},{15,7},{16,8},{17,9... | collective-permute-start | bytes 221192 | tf_op jit(solution)/shard_map/ppermute | solution.py:374
  51.2 11.2 %collective-permute-start.3 = (f32[16,1152]{1,0:T(8,128)}, f32[16,1152]{1,0:T(8,128)S(1)}, u32[]{:S(2)}, u32[]{:S(2)}) collective-permute-start(f32[16,1152]{1,0:T(8,128)} %get-tuple-element.15), channel_id=1, source_target_pairs={{0,8},{1,9},{2,10},{3,11},{4,12},{5,13},{6,14},{7,15},{8,16},{9,17... | collective-permute-start | bytes 221192 | tf_op jit(solution)/shard_map/ppermute | solution.py:373
  56.4 4.2 %collective-permute-start.4 = (f32[8,1152]{1,0:T(8,128)}, f32[8,1152]{1,0:T(8,128)S(1)}, u32[]{:S(2)}, u32[]{:S(2)}) collective-permute-start(f32[8,1152]{1,0:T(8,128)} %get-tuple-element.16), channel_id=1, source_target_pairs={{0,2},{2,4},{4,6},{6,7},{7,5},{5,3},{3,1},{1,0},{8,10},{10,12},{12... | collective-permute-start | bytes 110600 | tf_op jit(solution)/shard_map/ppermute | solution.py:375
  58.2 4.2 %collective-permute-start.5 = (f32[8,1152]{1,0:T(8,128)}, f32[8,1152]{1,0:T(8,128)S(1)}, u32[]{:S(2)}, u32[]{:S(2)}) collective-permute-start(f32[8,1152]{1,0:T(8,128)} %get-tuple-element.17), channel_id=1, source_target_pairs={{2,0},{4,2},{6,4},{7,6},{5,7},{3,5},{1,3},{0,1},{10,8},{12,10},{14... | collective-permute-start | bytes 110600 | tf_op jit(solution)/shard_map/ppermute | solution.py:376
  60.6 1.8 %copy-start.7 = (f32[8,1152]{1,0:T(8,128)}, f32[8,1152]{1,0:T(8,128)S(1)}, u32[]{:S(2)}) copy-start(f32[8,1152]{1,0:T(8,128)S(1)} %collective-permute-done.4.w_ref) | copy-start | bytes 110596
  62.4 0.6 copy-start.8
  62.4 0.6 copy-start.3
  62.4 0.7 copy-start.4
